TPU v7x, 256 devices: a whole 4x4x8 slice. The times are simulated.
256 devices in a mesh: arcs: 2 (over z_lo), trow: 8 (over y, core), tcol: 16 (over x, z_hi).
Axes of the slice: x: 4, y: 4, z: 8 (z_hi: 4, z_lo: 2; z = z_hi * 2 + z_lo), core: 2. Of those that a mesh axis runs over, the one named last changes fastest.
Arguments:
- design: bfloat16 [4096, 12288], P(('arcs', 'tcol'), 'trow'), may hold values from -6 to 6
- observed: float32 [4096], P(('arcs', 'tcol')), may hold values from -6 to 6
- arc_counts: int32 [128], P(('arcs', 'tcol')), may hold values from 2 to 32
- arc_weight: float32 [128], P(('arcs', 'tcol')), may hold values from 0.3 to 3
Outputs:
- gram: float32 [12288, 12288], P('trow', ('arcs', 'tcol'))
- rhs: float32 [12288], P('trow')
Inputs may be any that keep to these rules, and one draw needn't show every extreme that they name: `arc_counts`: each arc has at least two valid observations.
All inputs are finite; a program needn't handle non-finite values.
Results may differ from a plain program's by a relative error of at most 0.0055.
Values may be sent and summed in bfloat16 or wider, within the bound.
No kernel may reach another device: no remote copies, remote signals or barrier semaphores. Data moves between devices by JAX's collectives and lax.ppermute only.
A program may use at most 192 MiB of HBM per device.

v0:
```python
import jax
import jax.numpy as jnp
from jax import lax
from jax.sharding import PartitionSpec as P


def from_everyone(x, axis):
    devices = lax.axis_size(axis)
    return lax.all_to_all(jnp.broadcast_to(x[None], (devices, *x.shape)), axis, 0, 0, tiled=True)


def over_copies(x, axis):
    return from_everyone(x, axis).sum(axis=0)


def cut_along(x, dim, devices):
    dims = x.shape
    blocks = x.reshape(*dims[:dim], devices, dims[dim] // devices, *dims[dim + 1 :])
    return jnp.moveaxis(blocks, dim, 0)


def sum_at_owner(x, axis, dim):
    blocks = cut_along(x, dim, lax.axis_size(axis))
    arrived = lax.all_to_all(blocks, axis, split_axis=0, concat_axis=0, tiled=True)
    return arrived.astype(jnp.float32).sum(axis=0)


def fold_with(right, piece):
    return lax.dot_general(
        piece, right, (((0,), (0,)), ((), ())), preferred_element_type=jnp.float32
    )


def local(design, observed, arc_counts, arc_weight):
    row_count, col_width = design.shape
    arc_total = arc_counts.shape[0]
    arc_len = row_count // arc_total
    slot_index = lax.broadcasted_iota(jnp.int32, (arc_total, arc_len), 1)
    valid_mask = (slot_index < arc_counts[:, None]).astype(jnp.float32)
    counts_float = arc_counts.astype(jnp.float32)
    factor = valid_mask * jnp.sqrt(arc_weight)[:, None]
    blocks = design.reshape(arc_total, arc_len, col_width).astype(jnp.float32)
    column_mean = jnp.sum(valid_mask[:, :, None] * blocks, axis=1) / counts_float[:, None]
    centered = (
        (factor[:, :, None] * (blocks - column_mean[:, None, :]))
        .reshape(row_count, col_width)
        .astype(jnp.bfloat16)
    )
    series = observed.reshape(arc_total, arc_len)
    series_mean = jnp.sum(valid_mask * series, axis=1) / counts_float
    weighted = (factor * (series - series_mean[:, None])).reshape(row_count)
    arc_devices = lax.axis_size("arcs")
    tcol_devices = lax.axis_size("tcol")
    obs_total = row_count * arc_devices * tcol_devices
    rhs_part = jnp.dot(weighted, centered.astype(jnp.float32), precision=lax.Precision.HIGHEST)
    rhs = over_copies(rhs_part, ("arcs", "tcol")) * obs_total ** (-0.5)
    every_coef = lax.all_gather(centered, "trow", axis=1, tiled=True)
    full_width = every_coef.shape[1]
    narrow = full_width // (arc_devices * tcol_devices)
    shaped = every_coef.reshape(row_count, arc_devices, tcol_devices, narrow)
    moved = lax.all_to_all(shaped, "tcol", split_axis=2, concat_axis=0, tiled=True)
    right = moved.reshape(row_count * tcol_devices, arc_devices * narrow)
    partial_value = fold_with(right, lax.all_gather(centered, "tcol", axis=0, tiled=True))
    tile = sum_at_owner(partial_value.astype(jnp.bfloat16), "arcs", 1)
    gram = tile * (1.0 / obs_total)
    return (gram, rhs)


def solution(mesh):
    return jax.shard_map(
        local,
        mesh=mesh,
        in_specs=(
            P(("arcs", "tcol"), "trow"),
            P(("arcs", "tcol")),
            P(("arcs", "tcol")),
            P(("arcs", "tcol")),
        ),
        out_specs=(P("trow", ("arcs", "tcol")), P("trow")),
        check_vma=False,
    )
```

profile of v0, /device:TPU:1, one launch (start us, length us, event | category | flops | bytes accessed | tf_op | source)
XLA Modules:
  0.0 264.2 jit_solution(5195800618479505239)
XLA Ops:
  7.2 0.7 fusion.4
  7.9 0.7 convert_element_type.33
  8.6 0.7 reshape.101
  9.3 0.7 sqrt.3
  10.0 1.4 select_reduce_fusion
  11.4 1.2 multiply_reduce_fusion
  12.7 1.9 fusion.3
  14.6 0.7 all-gather.3.cloned.1.call-update
  15.3 33.9 %all-gather.5.cloned.1.call-done = bf16[128,12288]{1,0:T(8,128)(2,1)} async-done(((bf16[128,1536]{1,0:T(8,128)(2,1)}), bf16[128,12288]{1,0:T(8,128)(2,1)}) %all-gather.5.cloned.1.call-update) | async-done | bytes 3145744 | tf_op jit(solution)/shard_map/all_gather | solution.py:57
  49.2 3.5 %copy.21 = bf16[128,12288]{0,1:T(8,128)(2,1)S(1)} copy(bf16[128,12288]{1,0:T(8,128)(2,1)} %all-gather.5.cloned.1.call-done) | data formatting | bytes 6291456 | tf_op jit(solution)/shard_map/all_gather | solution.py:57
  52.7 1.9 copy.22
  54.6 9.4 %all-to-all-start = ((bf16[128,2,16,384]{0,3,1,2:T(8,128)(2,1)}), bf16[128,2,16,384]{0,3,1,2:T(8,128)(2,1)S(1)}, u32[]{:S(2)}, u32[]{:S(2)}) async-start(bf16[128,2,16,384]{0,3,1,2:T(8,128)(2,1)} %copy.22), calls=%async_computation | async-start | bytes 6291456 | tf_op jit(solution)/shard_map/all_to_all | solution.py:61
  64.0 0.7 convert_divide_fusion
  65.3 0.9 convolution_reduce_fusion
  66.3 82.1 %all-to-all-done = bf16[128,2,16,384]{0,3,1,2:T(8,128)(2,1)S(1)} async-done(((bf16[128,2,16,384]{0,3,1,2:T(8,128)(2,1)}), bf16[128,2,16,384]{0,3,1,2:T(8,128)(2,1)S(1)}, u32[]{:S(2)}, u32[]{:S(2)}) %all-to-all-start) | async-done | bytes 3145760 | tf_op jit(solution)/shard_map/all_to_all | solution.py:61
  148.4 0.8 broadcast_in_dim.2
  149.2 10.1 %all-to-all-start.2 = ((f32[32,1,1536]{2,1,0:T(1,128)}), f32[32,1,1536]{2,1,0:T(1,128)S(1)}, u32[]{:S(2)}, u32[]{:S(2)}) async-start(f32[32,1,1536]{2,1,0:T(1,128)} %broadcast_in_dim.2), calls=%async_computation.2 | async-start | bytes 393216 | tf_op jit(solution)/shard_map/all_to_all | solution.py:9
  159.2 3.7 %copy.23 = bf16[16,128,2,1,384]{1,0,4,2,3:T(8,128)(2,1)} copy(bf16[16,128,2,1,384]{1,4,2,0,3:T(8,128)(2,1)S(1)} %bitcast.27) | data formatting | bytes 6291456 | tf_op jit(solution)/shard_map/all_to_all | solution.py:61
  163.0 51.0 %all-gather.3.cloned.1.call-done = bf16[2048,1536]{1,0:T(8,128)(2,1)} async-done(((bf16[128,1536]{1,0:T(8,128)(2,1)}), bf16[2048,1536]{1,0:T(8,128)(2,1)}) %all-gather.3.cloned.1.call-update) | async-done | bytes 6291472 | tf_op jit(solution)/shard_map/all_gather | solution.py:63
  213.9 9.5 %convolution_convert_fusion = bf16[1536,768]{0,1:T(8,128)(2,1)} fusion(bf16[2048,1536]{1,0:T(8,128)(2,1)} %all-gather.3.cloned.1.call-done, bf16[96,8,16,128]{3,2,1,0:T(8,128)(2,1)} %bitcast.29), kind=kOutput, calls=%fused_computation.1 | convolution fusion | flops 4833017856 | bytes 11796480 | tf_op jit(solution)/shard_map/dot_general | solution.py:29
  223.4 3.8 %all-to-all-start.1 = ((bf16[2,1536,384]{1,2,0:T(8,128)(2,1)}), bf16[2,1536,384]{1,2,0:T(8,128)(2,1)S(1)}, u32[]{:S(2)}, u32[]{:S(2)}) async-start(bf16[2,1536,384]{1,2,0:T(8,128)(2,1)} %bitcast.30), calls=%async_computation.1 | async-start | bytes 4718592 | tf_op jit(solution)/shard_map/all_to_all | solution.py:24
  227.4 0.6 broadcast_multiply_fusion.1
  228.0 26.8 %all-to-all-done.1 = bf16[2,1536,384]{1,2,0:T(8,128)(2,1)S(1)} async-done(((bf16[2,1536,384]{1,2,0:T(8,128)(2,1)}), bf16[2,1536,384]{1,2,0:T(8,128)(2,1)S(1)}, u32[]{:S(2)}, u32[]{:S(2)}) %all-to-all-start.1) | async-done | bytes 2359328 | tf_op jit(solution)/shard_map/all_to_all | solution.py:24
  255.4 2.0 copy.25
  (17 shorter events, 1.7 us)
Async XLA Ops:
  7.2 42.0 %all-gather.5.cloned.1.call-start = ((), (), s32[]{:S(2)}) async-start(), calls=%async_computation.4 | async-start | bytes 3538944 | tf_op jit(solution)/shard_map/all_gather | solution.py:57
  14.6 199.3 %all-gather.3.cloned.1.call-start = ((), (), s32[]{:S(2)}) async-start(), calls=%async_computation.3 | async-start | bytes 6684672 | tf_op jit(solution)/shard_map/all_gather | solution.py:63
  54.6 9.4 %copy-start.2 = (s32[4]{0:T(128)S(1)}, s32[4]{0:T(128)}, u32[]{:S(2)}) copy-start(s32[4]{0:T(128)} %param.6) | copy-start | bytes 52
  54.6 10.7 %copy-start = (bf16[128,1536]{1,0:T(8,128)(2,1)S(1)}, bf16[128,1536]{1,0:T(8,128)(2,1)}, u32[]{:S(2)}) copy-start(bf16[128,1536]{1,0:T(8,128)(2,1)} %fusion.3) | copy-start | bytes 1179652
  54.6 10.7 %copy-start.1 = (f32[128]{0:T(128)S(1)}, f32[128]{0:T(128)}, u32[]{:S(2)}) copy-start(f32[128]{0:T(128)} %param.5) | copy-start | bytes 1540
  54.6 93.8 %all-to-all-start = ((bf16[128,2,16,384]{0,3,1,2:T(8,128)(2,1)}), bf16[128,2,16,384]{0,3,1,2:T(8,128)(2,1)S(1)}, u32[]{:S(2)}, u32[]{:S(2)}) async-start(bf16[128,2,16,384]{0,3,1,2:T(8,128)(2,1)} %copy.22), calls=%async_computation | async-start | bytes 6291456 | tf_op jit(solution)/shard_map/all_to_all | solution.py:61
  149.2 74.3 %all-to-all-start.2 = ((f32[32,1,1536]{2,1,0:T(1,128)}), f32[32,1,1536]{2,1,0:T(1,128)S(1)}, u32[]{:S(2)}, u32[]{:S(2)}) async-start(f32[32,1,1536]{2,1,0:T(1,128)} %broadcast_in_dim.2), calls=%async_computation.2 | async-start | bytes 393216 | tf_op jit(solution)/shard_map/all_to_all | solution.py:9
  223.4 31.3 %all-to-all-start.1 = ((bf16[2,1536,384]{1,2,0:T(8,128)(2,1)}), bf16[2,1536,384]{1,2,0:T(8,128)(2,1)S(1)}, u32[]{:S(2)}, u32[]{:S(2)}) async-start(bf16[2,1536,384]{1,2,0:T(8,128)(2,1)} %bitcast.30), calls=%async_computation.1 | async-start | bytes 4718592 | tf_op jit(solution)/shard_map/all_to_all | solution.py:24
Sparse Core Ops, SparseCore 0:
  14.7 34.4 all-gather.4
  52.2 161.6 all-gather.2
where the time goes:
time: 265 us; the launch traced here: 264 us
  waiting for transfers between devices  194 us (73%)
  starting transfers between devices  23.3 us (9%)
  between operations  14.1 us (5%)
  local copies, waits for them, and re-layouts  14 us (5%)
  matrix products  10.4 us (4%)
  other arithmetic  7.85 us (3%)
    all_to_all x1, waiting for transfers between devices, local(): lax.all_to_all(shaped, 'tcol', split_axis=2, concat_axis=0, tiled=True)  82.1 us
    all_gather x1, waiting for transfers between devices, local(): lax.all_gather(centered, 'tcol', axis=0, tiled=True)  51 us
    all_gather x1, waiting for transfers between devices, local(): every_coef = lax.all_gather(centered, 'trow', axis=1, tiled=True)  33.9 us
    all_to_all x1, waiting for transfers between devices, sum_at_owner(): lax.all_to_all(blocks, axis, split_axis=0, concat_axis=0, tiled=True)  26.8 us
    all_to_all x1, starting transfers between devices, from_everyone(): lax.all_to_all(jnp.broadcast_to(x[None], (devices, *x.shape)), axis, 0, 0...  10.1 us
    dot_general x1, matrix products, fold_with(): lax.dot_general(piece, right, (((0,), (0,)), ((), ())), preferred_element...  9.51 us
    all_to_all x1, starting transfers between devices, local(): lax.all_to_all(shaped, 'tcol', split_axis=2, concat_axis=0, tiled=True)  9.38 us
  transfers between devices with their start and end apart: 5, of which 4 were waited for; matrix products, arithmetic and copies ran while one was open for 8% of the time, Pallas kernels for 0%

commit v1 on v0

--- a/solution.py
+++ b/solution.py
@@ -2,6 +2,28 @@
 import jax.numpy as jnp
 from jax import lax
 from jax.sharding import PartitionSpec as P
+
+
+def joined_along(pieces, dim):
+    lengths = list(pieces.shape[1:])
+    lengths[dim] *= pieces.shape[0]
+    return jnp.moveaxis(pieces, 0, dim).reshape(lengths)
+
+
+def gather_around(shard, axis, dim):
+    devices = lax.axis_size(axis)
+    pairs = [(i, (i + 1) % devices) for i in range(devices)]
+    back = [(b, a) for a, b in pairs]
+    lower, upper = ([], [])
+    for hop in range(devices - 1):
+        if hop % 2 == 0:
+            lower.append(lax.ppermute(lower[-1] if lower else shard, axis, pairs))
+        else:
+            upper.append(lax.ppermute(upper[-1] if upper else shard, axis, back))
+    tiles = jnp.stack([*lower[::-1], shard, *upper])
+    shift = lax.axis_index(axis) - len(lower)
+    tiles = tiles[(jnp.arange(devices) - shift) % devices]
+    return joined_along(tiles, dim)
 
 
 def from_everyone(x, axis):
@@ -54,7 +76,7 @@
     obs_total = row_count * arc_devices * tcol_devices
     rhs_part = jnp.dot(weighted, centered.astype(jnp.float32), precision=lax.Precision.HIGHEST)
     rhs = over_copies(rhs_part, ("arcs", "tcol")) * obs_total ** (-0.5)
-    every_coef = lax.all_gather(centered, "trow", axis=1, tiled=True)
+    every_coef = gather_around(centered, "trow", 1)
     full_width = every_coef.shape[1]
     narrow = full_width // (arc_devices * tcol_devices)
     shaped = every_coef.reshape(row_count, arc_devices, tcol_devices, narrow)

time: 265 us -> 245 us (0.925)
  the two profiles are of different devices: /device:TPU:1 before, /device:TPU:24 now
where the time goes in v1:
time: 245 us
  waiting for transfers between devices  163 us (67%)
  starting transfers between devices  24.9 us (10%)
  local copies, waits for them, and re-layouts  24.2 us (10%)
  between operations  14.1 us (6%)
  matrix products  10.4 us (4%)
  other arithmetic  7.86 us (3%)
    all_to_all x1, waiting for transfers between devices, local(): lax.all_to_all(shaped, 'tcol', split_axis=2, concat_axis=0, tiled=True)  113 us
    all_to_all x1, waiting for transfers between devices, sum_at_owner(): lax.all_to_all(blocks, axis, split_axis=0, concat_axis=0, tiled=True)  27.4 us
    ppermute x4, waiting for transfers between devices, gather_around(): lower.append(lax.ppermute(lower[-1] if lower else shard, axis, pairs))  22.9 us
    all_to_all x1, starting transfers between devices, local(): lax.all_to_all(shaped, 'tcol', split_axis=2, concat_axis=0, tiled=True)  11.2 us
    dot_general x1, matrix products, fold_with(): lax.dot_general(piece, right, (((0,), (0,)), ((), ())), preferred_element...  9.51 us
    unnamed x14, local copies, waits for them, and re-layouts  7.42 us
  transfers between devices with their start and end apart: 11, of which 6 were waited for; matrix products, arithmetic and copies ran while one was open for 13% of the time, Pallas kernels for 0%

profile of v1, /device:TPU:24, one launch (start us, length us, event | category | flops | bytes accessed | tf_op | source)
XLA Modules:
  0.0 244.9 jit_solution(1781045762818310576)
XLA Ops:
  10.0 1.4 select_reduce_fusion
  11.4 1.2 multiply_reduce_fusion
  12.7 1.9 fusion.3
  14.6 7.4 %collective-permute-done = bf16[128,1536]{1,0:T(8,128)(2,1)S(1)} collective-permute-done((bf16[128,1536]{1,0:T(8,128)(2,1)}, bf16[128,1536]{1,0:T(8,128)(2,1)S(1)}, u32[]{:S(2)}, u32[]{:S(2)}) %collective-permute-start) | collective-permute-done | bytes 393248 | tf_op jit(solution)/shard_map/ppermute | solution.py:20
  22.0 1.7 collective-permute-start.4
  23.8 5.5 %collective-permute-done.1 = bf16[128,1536]{1,0:T(8,128)(2,1)S(1)} collective-permute-done((bf16[128,1536]{1,0:T(8,128)(2,1)S(1)}, bf16[128,1536]{1,0:T(8,128)(2,1)S(1)}, u32[]{:S(2)}, u32[]{:S(2)}) %collective-permute-start.1) | collective-permute-done | bytes 393248 | tf_op jit(solution)/shard_map/ppermute | solution.py:20
  30.0 1.2 collective-permute-start.5
  31.2 5.2 %collective-permute-done.2 = bf16[128,1536]{1,0:T(8,128)(2,1)S(1)} collective-permute-done((bf16[128,1536]{1,0:T(8,128)(2,1)S(1)}, bf16[128,1536]{1,0:T(8,128)(2,1)S(1)}, u32[]{:S(2)}, u32[]{:S(2)}) %collective-permute-start.2) | collective-permute-done | bytes 393248 | tf_op jit(solution)/shard_map/ppermute | solution.py:20
  36.4 2.0 collective-permute-start.3
  38.8 4.8 %collective-permute-done.3 = bf16[128,1536]{1,0:T(8,128)(2,1)S(1)} collective-permute-done((bf16[128,1536]{1,0:T(8,128)(2,1)S(1)}, bf16[128,1536]{1,0:T(8,128)(2,1)S(1)}, u32[]{:S(2)}, u32[]{:S(2)}) %collective-permute-start.3) | collective-permute-done | bytes 393248 | tf_op jit(solution)/shard_map/ppermute | solution.py:20
  47.5 0.8 bitcast_dynamic-update-slice_fusion.2
  48.3 0.8 bitcast_dynamic-update-slice_fusion.1
  49.9 2.6 %gather_fusion = bf16[8,128,1536]{2,1,0:T(8,128)(2,1)S(1)} fusion(bf16[8,128,1536]{2,1,0:T(8,128)(2,1)} %bitcast_dynamic-update-slice_fusion, s32[1024]{0:T(1024)S(1)} %pad_clamp_fusion), kind=kCustom, calls=%fused_computation | custom fusion | bytes 6291488 | tf_op jit(solution)/shard_map/gather | solution.py:25
  52.5 2.8 %copy.17 = bf16[128,8,1536]{0,2,1:T(8,128)(2,1)} copy(bf16[128,8,1536]{2,0,1:T(8,128)(2,1)S(1)} %bitcast.47) | data formatting | bytes 6291456 | tf_op jit(solution)/shard_map/transpose | solution.py:10
  55.4 3.9 %copy.18 = bf16[128,2,16,384]{0,3,1,2:T(8,128)(2,1)} copy(bf16[128,2,16,384]{0,3,2,1:T(8,128)(2,1)} %bitcast.48) | data formatting | bytes 6291456 | tf_op jit(solution)/shard_map/reshape;reshape | solution.py:82
  59.2 11.2 %all-to-all-start = ((bf16[128,2,16,384]{0,3,1,2:T(8,128)(2,1)}), bf16[128,2,16,384]{0,3,1,2:T(8,128)(2,1)S(1)}, u32[]{:S(2)}, u32[]{:S(2)}) async-start(bf16[128,2,16,384]{0,3,1,2:T(8,128)(2,1)} %copy.18), calls=%async_computation | async-start | bytes 6291456 | tf_op jit(solution)/shard_map/all_to_all | solution.py:83
  71.8 0.9 convolution_reduce_fusion
  72.7 112.9 %all-to-all-done = bf16[128,2,16,384]{0,3,1,2:T(8,128)(2,1)S(1)} async-done(((bf16[128,2,16,384]{0,3,1,2:T(8,128)(2,1)}), bf16[128,2,16,384]{0,3,1,2:T(8,128)(2,1)S(1)}, u32[]{:S(2)}, u32[]{:S(2)}) %all-to-all-start) | async-done | bytes 3145760 | tf_op jit(solution)/shard_map/all_to_all | solution.py:83
  186.4 3.9 %all-to-all-start.2 = ((f32[32,1,1536]{2,1,0:T(1,128)}), f32[32,1,1536]{2,1,0:T(1,128)S(1)}, u32[]{:S(2)}, u32[]{:S(2)}) async-start(f32[32,1,1536]{2,1,0:T(1,128)} %broadcast_in_dim.2), calls=%async_computation.2 | async-start | bytes 393216 | tf_op jit(solution)/shard_map/all_to_all | solution.py:31
  190.2 3.7 %copy.19 = bf16[16,128,2,1,384]{1,0,4,2,3:T(8,128)(2,1)} copy(bf16[16,128,2,1,384]{1,4,2,0,3:T(8,128)(2,1)S(1)} %bitcast.46) | data formatting | bytes 6291456 | tf_op jit(solution)/shard_map/all_to_all | solution.py:83
  194.0 9.5 %convolution_convert_fusion = bf16[1536,768]{0,1:T(8,128)(2,1)} fusion(bf16[2048,1536]{1,0:T(8,128)(2,1)} %all-gather.2.cloned.1.call-done, bf16[96,8,16,128]{3,2,1,0:T(8,128)(2,1)} %bitcast.49), kind=kOutput, calls=%fused_computation.2 | convolution fusion | flops 4833017856 | bytes 11796480 | tf_op jit(solution)/shard_map/dot_general | solution.py:51
  203.5 3.8 %all-to-all-start.1 = ((bf16[2,1536,384]{1,2,0:T(8,128)(2,1)}), bf16[2,1536,384]{1,2,0:T(8,128)(2,1)S(1)}, u32[]{:S(2)}, u32[]{:S(2)}) async-start(bf16[2,1536,384]{1,2,0:T(8,128)(2,1)} %bitcast.50), calls=%async_computation.1 | async-start | bytes 4718592 | tf_op jit(solution)/shard_map/all_to_all | solution.py:46
  208.0 27.4 %all-to-all-done.1 = bf16[2,1536,384]{1,2,0:T(8,128)(2,1)S(1)} async-done(((bf16[2,1536,384]{1,2,0:T(8,128)(2,1)}), bf16[2,1536,384]{1,2,0:T(8,128)(2,1)S(1)}, u32[]{:S(2)}, u32[]{:S(2)}) %all-to-all-start.1) | async-done | bytes 2359328 | tf_op jit(solution)/shard_map/all_to_all | solution.py:46
  236.1 2.0 copy.21
  (39 shorter events, 12.2 us)
Async XLA Ops:
  7.2 186.8 %all-gather.2.cloned.1.call-start = ((), (), s32[]{:S(2)}) async-start(), calls=%async_computation.3 | async-start | bytes 6684672 | tf_op jit(solution)/shard_map/all_gather | solution.py:85
  14.6 32.1 %copy-start = (bf16[128,1536]{1,0:T(8,128)(2,1)S(1)}, bf16[128,1536]{1,0:T(8,128)(2,1)}, u32[]{:S(2)}) copy-start(bf16[128,1536]{1,0:T(8,128)(2,1)} %fusion.3) | copy-start | bytes 1179652
  14.6 7.4 %collective-permute-start = (bf16[128,1536]{1,0:T(8,128)(2,1)}, bf16[128,1536]{1,0:T(8,128)(2,1)S(1)}, u32[]{:S(2)}, u32[]{:S(2)}) collective-permute-start(bf16[128,1536]{1,0:T(8,128)(2,1)} %fusion.3), channel_id=1, source_target_pairs={{0,16},{16,32},{32,48},{48,64},{64,80},{80,96},{96,112},{112,0},{1... | collective-permute-start | bytes 1179656 | tf_op jit(solution)/shard_map/ppermute | solution.py:20
  22.0 7.2 %collective-permute-start.1 = (bf16[128,1536]{1,0:T(8,128)(2,1)S(1)}, bf16[128,1536]{1,0:T(8,128)(2,1)S(1)}, u32[]{:S(2)}, u32[]{:S(2)}) collective-permute-start(bf16[128,1536]{1,0:T(8,128)(2,1)S(1)} %collective-permute-done), channel_id=1, source_target_pairs={{0,16},{16,32},{32,48},{48,64},{64,80},{80,96},{96,112},{112,0},{1... | collective-permute-start | bytes 1179656 | tf_op jit(solution)/shard_map/ppermute | solution.py:20
  22.0 8.0 %collective-permute-start.4 = (bf16[128,1536]{1,0:T(8,128)(2,1)}, bf16[128,1536]{1,0:T(8,128)(2,1)S(1)}, u32[]{:S(2)}, u32[]{:S(2)}) collective-permute-start(bf16[128,1536]{1,0:T(8,128)(2,1)} %fusion.3), channel_id=1, source_target_pairs={{16,0},{32,16},{48,32},{64,48},{80,64},{96,80},{112,96},{0,112},{1... | collective-permute-start | bytes 1179656 | tf_op jit(solution)/shard_map/ppermute | solution.py:22
  29.2 7.2 %collective-permute-start.2 = (bf16[128,1536]{1,0:T(8,128)(2,1)S(1)}, bf16[128,1536]{1,0:T(8,128)(2,1)S(1)}, u32[]{:S(2)}, u32[]{:S(2)}) collective-permute-start(bf16[128,1536]{1,0:T(8,128)(2,1)S(1)} %collective-permute-done.1), channel_id=1, source_target_pairs={{0,16},{16,32},{32,48},{48,64},{64,80},{80,96},{96,112},{112,0},{1... | collective-permute-start | bytes 1179656 | tf_op jit(solution)/shard_map/ppermute | solution.py:20
  30.0 8.4 %collective-permute-start.5 = (bf16[128,1536]{1,0:T(8,128)(2,1)S(1)}, bf16[128,1536]{1,0:T(8,128)(2,1)S(1)}, u32[]{:S(2)}, u32[]{:S(2)}) collective-permute-start(bf16[128,1536]{1,0:T(8,128)(2,1)S(1)} %collective-permute-done.4), channel_id=1, source_target_pairs={{16,0},{32,16},{48,32},{64,48},{80,64},{96,80},{112,96},{0,112},{1... | collective-permute-start | bytes 1179656 | tf_op jit(solution)/shard_map/ppermute | solution.py:22
  36.4 7.2 %collective-permute-start.3 = (bf16[128,1536]{1,0:T(8,128)(2,1)S(1)}, bf16[128,1536]{1,0:T(8,128)(2,1)S(1)}, u32[]{:S(2)}, u32[]{:S(2)}) collective-permute-start(bf16[128,1536]{1,0:T(8,128)(2,1)S(1)} %collective-permute-done.2), channel_id=1, source_target_pairs={{0,16},{16,32},{32,48},{48,64},{64,80},{80,96},{96,112},{112,0},{1... | collective-permute-start | bytes 1179656 | tf_op jit(solution)/shard_map/ppermute | solution.py:20
  38.4 10.6 %collective-permute-start.6 = (bf16[128,1536]{1,0:T(8,128)(2,1)S(1)}, bf16[128,1536]{1,0:T(8,128)(2,1)S(1)}, u32[]{:S(2)}, u32[]{:S(2)}) collective-permute-start(bf16[128,1536]{1,0:T(8,128)(2,1)S(1)} %collective-permute-done.5), channel_id=1, source_target_pairs={{16,0},{32,16},{48,32},{64,48},{80,64},{96,80},{112,96},{0,112},{1... | collective-permute-start | bytes 1179656 | tf_op jit(solution)/shard_map/ppermute | solution.py:22
  59.2 11.2 %copy-start.2 = (s32[4]{0:T(128)S(1)}, s32[4]{0:T(128)}, u32[]{:S(2)}) copy-start(s32[4]{0:T(128)} %param.6) | copy-start | bytes 52
  59.2 12.5 %copy-start.1 = (f32[128]{0:T(128)S(1)}, f32[128]{0:T(128)}, u32[]{:S(2)}) copy-start(f32[128]{0:T(128)} %param.5) | copy-start | bytes 1540
  59.2 126.3 %all-to-all-start = ((bf16[128,2,16,384]{0,3,1,2:T(8,128)(2,1)}), bf16[128,2,16,384]{0,3,1,2:T(8,128)(2,1)S(1)}, u32[]{:S(2)}, u32[]{:S(2)}) async-start(bf16[128,2,16,384]{0,3,1,2:T(8,128)(2,1)} %copy.18), calls=%async_computation | async-start | bytes 6291456 | tf_op jit(solution)/shard_map/all_to_all | solution.py:83
  186.4 17.1 %all-to-all-start.2 = ((f32[32,1,1536]{2,1,0:T(1,128)}), f32[32,1,1536]{2,1,0:T(1,128)S(1)}, u32[]{:S(2)}, u32[]{:S(2)}) async-start(f32[32,1,1536]{2,1,0:T(1,128)} %broadcast_in_dim.2), calls=%async_computation.2 | async-start | bytes 393216 | tf_op jit(solution)/shard_map/all_to_all | solution.py:31
  203.5 32.0 %all-to-all-start.1 = ((bf16[2,1536,384]{1,2,0:T(8,128)(2,1)}), bf16[2,1536,384]{1,2,0:T(8,128)(2,1)S(1)}, u32[]{:S(2)}, u32[]{:S(2)}) async-start(bf16[2,1536,384]{1,2,0:T(8,128)(2,1)} %bitcast.50), calls=%async_computation.1 | async-start | bytes 4718592 | tf_op jit(solution)/shard_map/all_to_all | solution.py:46
Sparse Core Ops, SparseCore 0:
  14.7 154.6 all-gather.1
